TPU v7x, 32 devices: a whole 2x2x4 slice. The times are simulated.
32 devices in a mesh: patch: 16 (over z, y, x), pix: 2 (over core).
Axes of the slice: x: 2, y: 2, z: 4, core: 2. Of those that a mesh axis runs over, the one named last changes fastest.
Arguments:
- pixel_pos: float32 [2, 3072], P(None, ('patch', 'pix')), may hold values from -4 to 4
- pixel_view: float32 [3, 3072], P(None, ('patch', 'pix')), may hold values from -1 to 1
- observed: float32 [3072], P(('patch', 'pix')), may hold values from -6 to 6
- noise_scale: float32 [3072], P(('patch', 'pix')), may hold values from 0.5 to 2
- valid_mask: int32 [3072], P(('patch', 'pix')), may hold values 0 or 1
- patch_pos: float32 [2, 768], P(None, 'patch'), may hold values from -4 to 4
- patch_depth: float32 [768], P('patch'), may hold values from 0.3 to 1.5
- segment_ids: int32 [768], P('patch'), may hold values from 0 to 15, never falling along the last dimension, each value on 1 to 192 neighbouring positions
- seg_strike: float32 [16], replicated, may hold values from -3.140625 to 3.140625
- seg_dip: float32 [16], replicated, may hold values from 0.35 to 1.4
- slip_models: bfloat16 [768, 3, 128], P('patch'), may hold values from -0.8984375 to 0.8984375
Outputs:
- residual: float32 [3072, 128], P(('patch', 'pix'))
- misfit: float32 [128], replicated
Inputs may be any that keep to these rules, and one draw needn't show every extreme that they name: `segment_ids`: segment ids never fall along the patches.
All inputs are finite; a program needn't handle non-finite values. No bound on the sum of `valid_mask` on one device may be relied on, other than what follows from the above.
Results may differ from a plain program's by a relative error of at most 0.0003.
Values may be sent and summed in bfloat16 or wider, within the bound.
A program may use at most 64 MiB of HBM per device.

v0:
```python
import math
import jax
import jax.numpy as jnp
from jax import lax
from jax.sharding import PartitionSpec as P

two_pi = 2.0 * math.pi
mu_ratio = 0.5


def partner(value, axis, distance):
    mask = 2**distance
    pairs = [(source, source ^ mask) for source in range(lax.axis_size(axis))]
    return lax.ppermute(value, axis, pairs)


def point_green(pixel_pos, pixel_view, frame_rows):
    src_east = frame_rows[0][:, None]
    src_north = frame_rows[1][:, None]
    src_depth = frame_rows[2][:, None]
    sin_strike = frame_rows[3][:, None]
    cos_strike = frame_rows[4][:, None]
    sin_dip = frame_rows[5][:, None]
    cos_dip = frame_rows[6][:, None]
    east_gap = pixel_pos[0][None, :] - src_east
    north_gap = pixel_pos[1][None, :] - src_north
    along_x = east_gap * sin_strike + north_gap * cos_strike
    across = north_gap * sin_strike - east_gap * cos_strike
    depth_term = across * cos_dip + src_depth * sin_dip
    plane_term = across * sin_dip - src_depth * cos_dip
    radius = jnp.sqrt(along_x * along_x + across * across + src_depth * src_depth)
    over_r = 1.0 / radius
    over_r3 = over_r * over_r * over_r
    over_r5 = over_r3 * over_r * over_r
    over_rd = 1.0 / (radius + src_depth)
    base_term = over_r * over_rd * over_rd
    cubic_term = (3.0 * radius + src_depth) * over_r3 * over_rd * over_rd * over_rd
    square_term = (2.0 * radius + src_depth) * over_r3 * over_rd * over_rd
    term_one = mu_ratio * across * (base_term - along_x * along_x * cubic_term)
    term_two = mu_ratio * along_x * (base_term - across * across * cubic_term)
    term_three = mu_ratio * along_x * over_r3 - term_two
    term_four = -mu_ratio * along_x * across * square_term
    term_five = mu_ratio * (over_r * over_rd - along_x * along_x * square_term)
    scaled_q = 3.0 * plane_term * over_r5
    dip_mixed = sin_dip * cos_dip
    dip_square = sin_dip * sin_dip
    strike_x = -(scaled_q * along_x * along_x + term_one * sin_dip)
    strike_y = -(scaled_q * along_x * across + term_two * sin_dip)
    strike_z = -(scaled_q * along_x * src_depth + term_four * sin_dip)
    dip_x = -(scaled_q * along_x * depth_term - term_three * dip_mixed)
    dip_y = -(scaled_q * across * depth_term - term_one * dip_mixed)
    dip_z = -(scaled_q * src_depth * depth_term - term_five * dip_mixed)
    open_x = scaled_q * along_x * plane_term - term_three * dip_square
    open_y = scaled_q * across * plane_term - term_one * dip_square
    open_z = scaled_q * src_depth * plane_term - term_five * dip_square

    def project(comp_x, comp_y, comp_z):
        east_move = comp_x * sin_strike - comp_y * cos_strike
        north_move = comp_x * cos_strike + comp_y * sin_strike
        return (
            pixel_view[0][None, :] * east_move
            + pixel_view[1][None, :] * north_move
            + pixel_view[2][None, :] * comp_z
        ) / two_pi

    return jnp.stack(
        [
            project(strike_x, strike_y, strike_z),
            project(dip_x, dip_y, dip_z),
            project(open_x, open_y, open_z),
        ],
        axis=1,
    )


def local_frames(patch_pos, patch_depth, segment_ids, seg_strike, seg_dip):
    segment_count = seg_strike.shape[0]
    matches = segment_ids[:, None] == jnp.arange(segment_count, dtype=jnp.int32)[None, :]
    strike = jnp.sum(jnp.where(matches, seg_strike[None, :], 0.0), axis=1)
    dip_angle = jnp.sum(jnp.where(matches, seg_dip[None, :], 0.0), axis=1)
    return jnp.stack(
        [
            patch_pos[0],
            patch_pos[1],
            patch_depth,
            jnp.sin(strike),
            jnp.cos(strike),
            jnp.sin(dip_angle),
            jnp.cos(dip_angle),
        ],
        axis=0,
    )


def tile_product(site_pos, site_view, frame_rows, slip_table):
    pixel_count = site_pos.shape[1]
    green_tile = point_green(site_pos, site_view, frame_rows).astype(jnp.bfloat16)
    green_tile = green_tile.reshape(frame_rows.shape[1] * 3, pixel_count)
    return lax.dot_general(
        green_tile, slip_table, (((0,), (0,)), ((), ())), preferred_element_type=jnp.float32
    )


def patch_blocks(pixel_pos, pixel_view, frame_rows, slip_piece, running):
    patch_count = slip_piece.shape[0]
    samples = slip_piece.shape[2]
    block_len = min(patch_count, 640)
    full_blocks = patch_count // block_len
    remainder = patch_count - full_blocks * block_len
    head = full_blocks * block_len
    head_frames = frame_rows[:, :head].reshape(7, full_blocks, block_len).transpose(1, 0, 2)
    head_slip = slip_piece[:head].reshape(full_blocks, block_len * 3, samples)

    def add_tile(accum, block_items):
        return (accum + tile_product(pixel_pos, pixel_view, block_items[0], block_items[1]), None)

    running, _ = lax.scan(add_tile, running, (head_frames, head_slip))
    if remainder > 0:
        tail_slip = slip_piece[head:].reshape(remainder * 3, samples)
        running = running + tile_product(pixel_pos, pixel_view, frame_rows[:, head:], tail_slip)
    return running


def index_bit(level):
    return lax.axis_index("patch") // 2**level % 2 == 1


def join_pair(mine, other, upper, axis_dim):
    first = jnp.where(upper, other, mine)
    second = jnp.where(upper, mine, other)
    return jnp.concatenate([first, second], axis=axis_dim)


def per_device(
    pixel_pos,
    pixel_view,
    observed,
    noise_scale,
    valid_mask,
    patch_pos,
    patch_depth,
    segment_ids,
    seg_strike,
    seg_dip,
    slip_models,
):
    own_pixels = pixel_pos.shape[1]
    samples = slip_models.shape[2]
    frames = local_frames(patch_pos, patch_depth, segment_ids, seg_strike, seg_dip)
    total_bits = lax.axis_size("patch").bit_length() - 1
    low_count = (total_bits + 1) // 2
    group_slip = slip_models
    group_frames = frames
    for level in range(low_count):
        upper = index_bit(level)
        other_slip = partner(group_slip, "patch", level)
        other_frames = partner(group_frames, "patch", level)
        group_slip = join_pair(group_slip, other_slip, upper, 0)
        group_frames = join_pair(group_frames, other_frames, upper, 1)
    group_sites = jnp.concatenate([pixel_pos, pixel_view], axis=0)
    for level in range(low_count, total_bits):
        upper = index_bit(level)
        other_sites = partner(group_sites, "patch", level)
        group_sites = join_pair(group_sites, other_sites, upper, 1)
    site_groups = group_sites.shape[1] // own_pixels
    stacked = group_sites.reshape(5, site_groups, own_pixels).transpose(1, 0, 2)

    def one_group(block_sites):
        start = jnp.zeros((own_pixels, samples), jnp.float32)
        return patch_blocks(block_sites[:2], block_sites[2:], group_frames, group_slip, start)

    partial_value = lax.map(one_group, stacked).reshape(site_groups * own_pixels, samples)
    for level in range(total_bits - 1, low_count - 1, -1):
        upper = index_bit(level)
        half = partial_value.shape[0] // 2
        keep = jnp.where(upper, partial_value[half:], partial_value[:half])
        send = jnp.where(upper, partial_value[:half], partial_value[half:])
        partial_value = keep + partner(send, "patch", level)
    residual = (
        valid_mask.astype(jnp.float32)[:, None]
        * (partial_value - observed[:, None])
        / noise_scale[:, None]
    )
    own_sum = jnp.sum(residual * residual, axis=0)
    pixels = own_pixels * lax.axis_size("patch") * lax.axis_size("pix")
    misfit = lax.psum(own_sum, ("patch", "pix")) / pixels
    return (residual, misfit)


def solution(mesh):
    return jax.shard_map(
        per_device,
        mesh=mesh,
        in_specs=(
            P(None, ("patch", "pix")),
            P(None, ("patch", "pix")),
            P(("patch", "pix")),
            P(("patch", "pix")),
            P(("patch", "pix")),
            P(None, "patch"),
            P("patch"),
            P("patch"),
            P(),
            P(),
            P("patch", None, None),
        ),
        out_specs=(P(("patch", "pix"), None), P()),
        check_vma=False,
    )
```

profile of v0, /device:TPU:0, one launch (start us, length us, event | category | flops | bytes accessed | tf_op | source)
XLA Modules:
  0.0 74.1 jit_solution(12593632684655895281)
XLA Ops:
  0.6 3.0 %collective-permute-start.4 = (bf16[48,3,128]{2,0,1:T(8,128)(2,1)}, bf16[48,3,128]{2,0,1:T(8,128)(2,1)S(1)}, u32[]{:S(2)}, u32[]{:S(2)}) collective-permute-start(bf16[48,3,128]{2,0,1:T(8,128)(2,1)} %param.23), channel_id=1, source_target_pairs={{0,2},{2,0},{4,6},{6,4},{8,10},{10,8},{12,14},{14,12},{16,18},{18,... | collective-permute-start | bytes 110600 | tf_op jit(solution)/shard_map/ppermute | solution.py:14
  3.7 0.8 %select_reduce_fusion = (f32[48]{0:T(128)S(1)}, f32[48]{0:T(128)S(1)}) fusion(f32[16]{0:T(128)} %param.22, s32[48]{0:T(128)} %param.20, f32[16]{0:T(128)} %param.21), kind=kLoop, calls=%fused_computation.120 | loop fusion | flops 3744 | bytes 704 | tf_op jit(solution)/shard_map/reduce_sum | solution.py:80
  4.5 0.7 copy-done.3
  5.2 0.1 collective-permute-start.2
  5.3 0.6 copy-done.1
  5.9 1.6 %collective-permute-start = (f32[5,96]{1,0:T(8,128)S(1)}, f32[5,96]{1,0:T(8,128)S(1)}, u32[]{:S(2)}, u32[]{:S(2)}) collective-permute-start(f32[5,96]{1,0:T(8,128)S(1)} %pad_maximum_fusion.5), channel_id=1, source_target_pairs={{0,8},{2,10},{4,12},{6,14},{8,0},{10,2},{12,4},{14,6},{16,24},{18,... | collective-permute-start | bytes 5768 | tf_op jit(solution)/shard_map/ppermute | solution.py:14
  7.5 1.4 %collective-permute-done.2 = f32[7,48]{1,0:T(8,128)S(1)} collective-permute-done((f32[7,48]{1,0:T(8,128)S(1)}, f32[7,48]{1,0:T(8,128)S(1)}, u32[]{:S(2)}, u32[]{:S(2)}) %collective-permute-start.2) | collective-permute-done | bytes 1376 | tf_op jit(solution)/shard_map/ppermute | solution.py:14
  8.9 0.1 pad_maximum_fusion.6
  9.0 1.5 %collective-permute-start.3 = (f32[7,96]{1,0:T(8,128)S(1)}, f32[7,96]{1,0:T(8,128)S(1)}, u32[]{:S(2)}, u32[]{:S(2)}) collective-permute-start(f32[7,96]{1,0:T(8,128)S(1)} %pad_maximum_fusion.6), channel_id=1, source_target_pairs={{0,4},{2,6},{4,0},{6,2},{8,12},{10,14},{12,8},{14,10},{16,20},{18,... | collective-permute-start | bytes 8072 | tf_op jit(solution)/shard_map/ppermute | solution.py:14
  10.6 2.6 %collective-permute-start.1 = (f32[5,192]{1,0:T(8,128)S(1)}, f32[5,192]{1,0:T(8,128)S(1)}, u32[]{:S(2)}, u32[]{:S(2)}) collective-permute-start(f32[5,192]{1,0:T(8,128)S(1)} %pad_maximum_fusion.4), channel_id=1, source_target_pairs={{0,16},{2,18},{4,20},{6,22},{8,24},{10,26},{12,28},{14,30},{16,0},... | collective-permute-start | bytes 11528 | tf_op jit(solution)/shard_map/ppermute | solution.py:14
  13.2 0.1 multiply_bitcast_fusion
  13.3 0.1 multiply_bitcast_fusion.1
  13.5 1.6 %collective-permute-done.1 = f32[5,192]{1,0:T(8,128)S(1)} collective-permute-done((f32[5,192]{1,0:T(8,128)S(1)}, f32[5,192]{1,0:T(8,128)S(1)}, u32[]{:S(2)}, u32[]{:S(2)}) %collective-permute-start.1) | collective-permute-done | bytes 3872 | tf_op jit(solution)/shard_map/ppermute | solution.py:14
  15.2 0.7 collective-permute-start.5
  16.0 0.1 reshape.2726
  16.0 3.6 %collective-permute-done.5 = bf16[96,3,128]{2,0,1:T(8,128)(2,1)S(1)} collective-permute-done((bf16[96,3,128]{2,0,1:T(8,128)(2,1)S(1)}, bf16[96,3,128]{2,0,1:T(8,128)(2,1)S(1)}, u32[]{:S(2)}, u32[]{:S(2)}) %collective-permute-start.5) | collective-permute-done | bytes 73760 | tf_op jit(solution)/shard_map/ppermute | solution.py:14
  19.7 3.4 %while.11 = (s32[]{:T(128)}, f32[4,96,128]{2,1,0:T(8,128)S(1)}, f32[4,5,96]{2,0,1:T(4,128)S(1)}, f32[7,192]{1,0:T(8,128)S(1)}, f32[192,1]{0,1:T(1,128)S(1)}, /*i...) while((s32[]{:T(128)}, f32[4,96,128]{2,1,0:T(8,128)S(1)}, ...), condition=%wide.region_3.4_spmd, body=%wide.region_2.3_spmd.sunk | while | flops 16626054 | bytes 485213 | solution.py:172
  19.8 0.5 fusion.98
  20.3 0.2 fusion.99
  20.6 0.5 fusion.98
  21.2 0.2 fusion.99
  21.5 0.5 fusion.98
  22.0 0.2 fusion.99
  22.3 0.5 fusion.98
  22.9 0.2 fusion.99
  23.1 2.7 %collective-permute-start.6 = (f32[192,128]{1,0:T(8,128)S(1)}, f32[192,128]{1,0:T(8,128)S(1)}, u32[]{:S(2)}, u32[]{:S(2)}) collective-permute-start(f32[192,128]{1,0:T(8,128)S(1)} %bitcast.102), channel_id=1, source_target_pairs={{0,16},{2,18},{4,20},{6,22},{8,24},{10,26},{12,28},{14,30},{16,0},... | collective-permute-start | bytes 294920 | tf_op jit(solution)/shard_map/ppermute | solution.py:14
  25.8 2.9 %collective-permute-done.6 = f32[192,128]{1,0:T(8,128)S(1)} collective-permute-done((f32[192,128]{1,0:T(8,128)S(1)}, f32[192,128]{1,0:T(8,128)S(1)}, u32[]{:S(2)}, u32[]{:S(2)}) %collective-permute-start.6) | collective-permute-done | bytes 98336 | tf_op jit(solution)/shard_map/ppermute | solution.py:14
  28.8 2.2 %collective-permute-start.7 = (f32[96,128]{1,0:T(8,128)S(1)}, f32[96,128]{1,0:T(8,128)S(1)}, u32[]{:S(2)}, u32[]{:S(2)}) collective-permute-start(f32[96,128]{1,0:T(8,128)S(1)} %slice_select_fusion.2), channel_id=1, source_target_pairs={{0,8},{2,10},{4,12},{6,14},{8,0},{10,2},{12,4},{14,6},{16,24},{18,... | collective-permute-start | bytes 147464 | tf_op jit(solution)/shard_map/ppermute | solution.py:14
  31.0 2.1 %collective-permute-done.7 = f32[96,128]{1,0:T(8,128)S(1)} collective-permute-done((f32[96,128]{1,0:T(8,128)S(1)}, f32[96,128]{1,0:T(8,128)S(1)}, u32[]{:S(2)}, u32[]{:S(2)}) %collective-permute-start.7) | collective-permute-done | bytes 49184 | tf_op jit(solution)/shard_map/ppermute | solution.py:14
  33.0 0.7 multiply_reduce_fusion
  33.8 39.8 %psum.7 = f32[128]{0:T(128)S(1)} all-reduce(f32[128]{0:T(128)S(1)} %get-tuple-element.127), channel_id=1, replica_groups=mesh['patch'=16,'pix'=2] {'patch','pix'}, use_global_device_ids=true, to_apply=%region_5.6 | all-reduce | flops 128 | bytes 1024 | tf_op jit(solution)/shard_map/psum | solution.py:186
  73.6 0.5 broadcast_multiply_fusion.2
  (49 shorter events, 0.8 us)
Async XLA Ops:
  0.6 14.6 %collective-permute-start.4 = (bf16[48,3,128]{2,0,1:T(8,128)(2,1)}, bf16[48,3,128]{2,0,1:T(8,128)(2,1)S(1)}, u32[]{:S(2)}, u32[]{:S(2)}) collective-permute-start(bf16[48,3,128]{2,0,1:T(8,128)(2,1)} %param.23), channel_id=1, source_target_pairs={{0,2},{2,0},{4,6},{6,4},{8,10},{10,8},{12,14},{14,12},{16,18},{18,... | collective-permute-start | bytes 110600 | tf_op jit(solution)/shard_map/ppermute | solution.py:14
  4.5 0.7 copy-start.3
  4.5 0.7 copy-start.6
  5.2 0.7 copy-start.1
  5.2 0.7 copy-start.2
  5.2 3.7 %collective-permute-start.2 = (f32[7,48]{1,0:T(8,128)S(1)}, f32[7,48]{1,0:T(8,128)S(1)}, u32[]{:S(2)}, u32[]{:S(2)}) collective-permute-start(f32[7,48]{1,0:T(8,128)S(1)} %stack.24), channel_id=1, source_target_pairs={{0,2},{2,0},{4,6},{6,4},{8,10},{10,8},{12,14},{14,12},{16,18},{18,... | collective-permute-start | bytes 4040 | tf_op jit(solution)/shard_map/ppermute | solution.py:14
  5.9 4.6 %collective-permute-start = (f32[5,96]{1,0:T(8,128)S(1)}, f32[5,96]{1,0:T(8,128)S(1)}, u32[]{:S(2)}, u32[]{:S(2)}) collective-permute-start(f32[5,96]{1,0:T(8,128)S(1)} %pad_maximum_fusion.5), channel_id=1, source_target_pairs={{0,8},{2,10},{4,12},{6,14},{8,0},{10,2},{12,4},{14,6},{16,24},{18,... | collective-permute-start | bytes 5768 | tf_op jit(solution)/shard_map/ppermute | solution.py:14
  9.0 4.2 %collective-permute-start.3 = (f32[7,96]{1,0:T(8,128)S(1)}, f32[7,96]{1,0:T(8,128)S(1)}, u32[]{:S(2)}, u32[]{:S(2)}) collective-permute-start(f32[7,96]{1,0:T(8,128)S(1)} %pad_maximum_fusion.6), channel_id=1, source_target_pairs={{0,4},{2,6},{4,0},{6,2},{8,12},{10,14},{12,8},{14,10},{16,20},{18,... | collective-permute-start | bytes 8072 | tf_op jit(solution)/shard_map/ppermute | solution.py:14
  10.6 4.6 %collective-permute-start.1 = (f32[5,192]{1,0:T(8,128)S(1)}, f32[5,192]{1,0:T(8,128)S(1)}, u32[]{:S(2)}, u32[]{:S(2)}) collective-permute-start(f32[5,192]{1,0:T(8,128)S(1)} %pad_maximum_fusion.4), channel_id=1, source_target_pairs={{0,16},{2,18},{4,20},{6,22},{8,24},{10,26},{12,28},{14,30},{16,0},... | collective-permute-start | bytes 11528 | tf_op jit(solution)/shard_map/ppermute | solution.py:14
  13.3 1.9 %copy-start = (bf16[48,3,128]{2,0,1:T(8,128)(2,1)S(1)}, bf16[48,3,128]{2,0,1:T(8,128)(2,1)}, u32[]{:S(2)}) copy-start(bf16[48,3,128]{2,0,1:T(8,128)(2,1)} %param.23) | copy-start | bytes 110596
  15.2 4.4 %collective-permute-start.5 = (bf16[96,3,128]{2,0,1:T(8,128)(2,1)S(1)}, bf16[96,3,128]{2,0,1:T(8,128)(2,1)S(1)}, u32[]{:S(2)}, u32[]{:S(2)}) collective-permute-start(bf16[96,3,128]{2,0,1:T(8,128)(2,1)S(1)} %pad_maximum_fusion.1), channel_id=1, source_target_pairs={{0,4},{2,6},{4,0},{6,2},{8,12},{10,14},{12,8},{14,10},{16,20},{18,... | collective-permute-start | bytes 221192 | tf_op jit(solution)/shard_map/ppermute | solution.py:14
  23.1 5.6 %collective-permute-start.6 = (f32[192,128]{1,0:T(8,128)S(1)}, f32[192,128]{1,0:T(8,128)S(1)}, u32[]{:S(2)}, u32[]{:S(2)}) collective-permute-start(f32[192,128]{1,0:T(8,128)S(1)} %bitcast.102), channel_id=1, source_target_pairs={{0,16},{2,18},{4,20},{6,22},{8,24},{10,26},{12,28},{14,30},{16,0},... | collective-permute-start | bytes 294920 | tf_op jit(solution)/shard_map/ppermute | solution.py:14
  28.7 2.2 %copy-start.7 = (s32[96]{0:T(128)S(1)}, s32[96]{0:T(128)}, u32[]{:S(2)}) copy-start(s32[96]{0:T(128)} %param.17) | copy-start | bytes 1156
  28.8 4.3 %copy-start.4 = (f32[96]{0:T(128)S(1)}, f32[96]{0:T(128)}, u32[]{:S(2)}) copy-start(f32[96]{0:T(128)} %param.16) | copy-start | bytes 1156
  28.8 4.2 %copy-start.5 = (f32[96]{0:T(128)S(1)}, f32[96]{0:T(128)}, u32[]{:S(2)}) copy-start(f32[96]{0:T(128)} %param.15) | copy-start | bytes 1156
  28.8 4.2 %collective-permute-start.7 = (f32[96,128]{1,0:T(8,128)S(1)}, f32[96,128]{1,0:T(8,128)S(1)}, u32[]{:S(2)}, u32[]{:S(2)}) collective-permute-start(f32[96,128]{1,0:T(8,128)S(1)} %slice_select_fusion.2), channel_id=1, source_target_pairs={{0,8},{2,10},{4,12},{6,14},{8,0},{10,2},{12,4},{14,6},{16,24},{18,... | collective-permute-start | bytes 147464 | tf_op jit(solution)/shard_map/ppermute | solution.py:14
where the time goes:
time: 74.4 us; the launch traced here: 74.1 us
  blocking collectives  39.8 us (53%)
  starting transfers between devices  14.3 us (19%)
  waiting for transfers between devices  11.6 us (16%)
  other arithmetic  4.89 us (7%)
  local copies, waits for them, and re-layouts  1.55 us (2%)
  matrix products  0.95 us (1%)
  between operations  0.75 us (1%)
    psum x1, blocking collectives, per_device(): misfit = lax.psum(own_sum, ('patch', 'pix')) / pixels  39.8 us
    ppermute x8, starting transfers between devices, partner(): return lax.ppermute(value, axis, pairs)  14.3 us
    ppermute x8, waiting for transfers between devices, partner(): return lax.ppermute(value, axis, pairs)  11.6 us
    another operation x4, other arithmetic  2.11 us
  transfers between devices with their start and end apart: 8, of which 5 were waited for; matrix products, arithmetic and copies ran while one was open for 2% of the time, Pallas kernels for 0%

commit v1 on v0

--- a/solution.py
+++ b/solution.py
@@ -183,7 +183,7 @@
     )
     own_sum = jnp.sum(residual * residual, axis=0)
     pixels = own_pixels * lax.axis_size("patch") * lax.axis_size("pix")
-    misfit = lax.psum(own_sum, ("patch", "pix")) / pixels
+    misfit = lax.psum(lax.psum(own_sum, "pix"), "patch") / pixels
     return (residual, misfit)
 
 

time: 74.4 us -> 78.9 us (1.060)
  blocking collectives: 39.8 us -> 44.3 us
    psum x1 -> x2, blocking collectives: 39.8 us -> 44.3 us  [per_device(): misfit = lax.psum(lax.psum(own_sum, 'pix'), 'patch') / pixels]
where the time goes in v1:
time: 78.9 us; the launch traced here: 78.6 us
  blocking collectives  44.3 us (56%)
  starting transfers between devices  14.3 us (18%)
  waiting for transfers between devices  11.6 us (15%)
  other arithmetic  4.89 us (6%)
  local copies, waits for them, and re-layouts  1.55 us (2%)
  matrix products  0.95 us (1%)
    psum x2, blocking collectives, per_device(): misfit = lax.psum(lax.psum(own_sum, 'pix'), 'patch') / pixels  44.3 us
    ppermute x8, starting transfers between devices, partner(): return lax.ppermute(value, axis, pairs)  14.3 us
    ppermute x8, waiting for transfers between devices, partner(): return lax.ppermute(value, axis, pairs)  11.6 us
    another operation x4, other arithmetic  2.11 us
  transfers between devices with their start and end apart: 8, of which 5 were waited for; matrix products, arithmetic and copies ran while one was open for 2% of the time, Pallas kernels for 0%

profile of v1, /device:TPU:0, one launch (start us, length us, event | category | flops | bytes accessed | tf_op | source)
XLA Modules:
  0.0 78.6 jit_solution(6466675571411474175)
XLA Ops:
  0.6 3.0 %collective-permute-start.4 = (bf16[48,3,128]{2,0,1:T(8,128)(2,1)}, bf16[48,3,128]{2,0,1:T(8,128)(2,1)S(1)}, u32[]{:S(2)}, u32[]{:S(2)}) collective-permute-start(bf16[48,3,128]{2,0,1:T(8,128)(2,1)} %param.23), channel_id=1, source_target_pairs={{0,2},{2,0},{4,6},{6,4},{8,10},{10,8},{12,14},{14,12},{16,18},{18,... | collective-permute-start | bytes 110600 | tf_op jit(solution)/shard_map/ppermute | solution.py:14
  3.7 0.8 select_reduce_fusion
  4.5 0.7 copy-done.3
  5.2 0.1 collective-permute-start.2
  5.3 0.6 copy-done.1
  5.9 1.6 %collective-permute-start = (f32[5,96]{1,0:T(8,128)S(1)}, f32[5,96]{1,0:T(8,128)S(1)}, u32[]{:S(2)}, u32[]{:S(2)}) collective-permute-start(f32[5,96]{1,0:T(8,128)S(1)} %pad_maximum_fusion.5), channel_id=1, source_target_pairs={{0,8},{2,10},{4,12},{6,14},{8,0},{10,2},{12,4},{14,6},{16,24},{18,... | collective-permute-start | bytes 5768 | tf_op jit(solution)/shard_map/ppermute | solution.py:14
  7.5 1.4 %collective-permute-done.2 = f32[7,48]{1,0:T(8,128)S(1)} collective-permute-done((f32[7,48]{1,0:T(8,128)S(1)}, f32[7,48]{1,0:T(8,128)S(1)}, u32[]{:S(2)}, u32[]{:S(2)}) %collective-permute-start.2) | collective-permute-done | bytes 1376 | tf_op jit(solution)/shard_map/ppermute | solution.py:14
  8.9 0.1 pad_maximum_fusion.6
  9.0 1.5 %collective-permute-start.3 = (f32[7,96]{1,0:T(8,128)S(1)}, f32[7,96]{1,0:T(8,128)S(1)}, u32[]{:S(2)}, u32[]{:S(2)}) collective-permute-start(f32[7,96]{1,0:T(8,128)S(1)} %pad_maximum_fusion.6), channel_id=1, source_target_pairs={{0,4},{2,6},{4,0},{6,2},{8,12},{10,14},{12,8},{14,10},{16,20},{18,... | collective-permute-start | bytes 8072 | tf_op jit(solution)/shard_map/ppermute | solution.py:14
  10.6 2.6 %collective-permute-start.1 = (f32[5,192]{1,0:T(8,128)S(1)}, f32[5,192]{1,0:T(8,128)S(1)}, u32[]{:S(2)}, u32[]{:S(2)}) collective-permute-start(f32[5,192]{1,0:T(8,128)S(1)} %pad_maximum_fusion.4), channel_id=1, source_target_pairs={{0,16},{2,18},{4,20},{6,22},{8,24},{10,26},{12,28},{14,30},{16,0},... | collective-permute-start | bytes 11528 | tf_op jit(solution)/shard_map/ppermute | solution.py:14
  13.2 0.1 multiply_bitcast_fusion
  13.5 1.6 %collective-permute-done.1 = f32[5,192]{1,0:T(8,128)S(1)} collective-permute-done((f32[5,192]{1,0:T(8,128)S(1)}, f32[5,192]{1,0:T(8,128)S(1)}, u32[]{:S(2)}, u32[]{:S(2)}) %collective-permute-start.1) | collective-permute-done | bytes 3872 | tf_op jit(solution)/shard_map/ppermute | solution.py:14
  15.2 0.7 collective-permute-start.5
  16.0 0.1 reshape.2726
  16.0 3.6 %collective-permute-done.5 = bf16[96,3,128]{2,0,1:T(8,128)(2,1)S(1)} collective-permute-done((bf16[96,3,128]{2,0,1:T(8,128)(2,1)S(1)}, bf16[96,3,128]{2,0,1:T(8,128)(2,1)S(1)}, u32[]{:S(2)}, u32[]{:S(2)}) %collective-permute-start.5) | collective-permute-done | bytes 73760 | tf_op jit(solution)/shard_map/ppermute | solution.py:14
  19.7 3.4 %while.11 = (s32[]{:T(128)}, f32[4,96,128]{2,1,0:T(8,128)S(1)}, f32[4,5,96]{2,0,1:T(4,128)S(1)}, f32[7,192]{1,0:T(8,128)S(1)}, f32[192,1]{0,1:T(1,128)S(1)}, /*i...) while((s32[]{:T(128)}, f32[4,96,128]{2,1,0:T(8,128)S(1)}, ...), condition=%wide.region_3.4_spmd, body=%wide.region_2.3_spmd.sunk | while | flops 16626054 | bytes 485213 | solution.py:172
  19.8 0.5 fusion.98
  20.3 0.2 fusion.99
  20.6 0.5 fusion.98
  21.2 0.2 fusion.99
  21.5 0.5 fusion.98
  22.0 0.2 fusion.99
  22.3 0.5 fusion.98
  22.9 0.2 fusion.99
  23.1 2.7 %collective-permute-start.6 = (f32[192,128]{1,0:T(8,128)S(1)}, f32[192,128]{1,0:T(8,128)S(1)}, u32[]{:S(2)}, u32[]{:S(2)}) collective-permute-start(f32[192,128]{1,0:T(8,128)S(1)} %bitcast.102), channel_id=1, source_target_pairs={{0,16},{2,18},{4,20},{6,22},{8,24},{10,26},{12,28},{14,30},{16,0},... | collective-permute-start | bytes 294920 | tf_op jit(solution)/shard_map/ppermute | solution.py:14
  25.8 2.9 %collective-permute-done.6 = f32[192,128]{1,0:T(8,128)S(1)} collective-permute-done((f32[192,128]{1,0:T(8,128)S(1)}, f32[192,128]{1,0:T(8,128)S(1)}, u32[]{:S(2)}, u32[]{:S(2)}) %collective-permute-start.6) | collective-permute-done | bytes 98336 | tf_op jit(solution)/shard_map/ppermute | solution.py:14
  28.8 2.2 %collective-permute-start.7 = (f32[96,128]{1,0:T(8,128)S(1)}, f32[96,128]{1,0:T(8,128)S(1)}, u32[]{:S(2)}, u32[]{:S(2)}) collective-permute-start(f32[96,128]{1,0:T(8,128)S(1)} %slice_select_fusion.2), channel_id=1, source_target_pairs={{0,8},{2,10},{4,12},{6,14},{8,0},{10,2},{12,4},{14,6},{16,24},{18,... | collective-permute-start | bytes 147464 | tf_op jit(solution)/shard_map/ppermute | solution.py:14
  31.0 2.1 %collective-permute-done.7 = f32[96,128]{1,0:T(8,128)S(1)} collective-permute-done((f32[96,128]{1,0:T(8,128)S(1)}, f32[96,128]{1,0:T(8,128)S(1)}, u32[]{:S(2)}, u32[]{:S(2)}) %collective-permute-start.7) | collective-permute-done | bytes 49184 | tf_op jit(solution)/shard_map/ppermute | solution.py:14
  33.0 0.7 multiply_reduce_fusion
  33.8 2.4 %psum.14 = f32[128]{0:T(128)S(1)} all-reduce(f32[128]{0:T(128)S(1)} %get-tuple-element.127), channel_id=1, replica_groups=mesh['patch'=16,'pix'=2] {'pix'}, use_global_device_ids=true, to_apply=%region_5.6 | all-reduce | flops 128 | bytes 1024 | tf_op jit(solution)/shard_map/psum | solution.py:186
  36.2 41.9 %psum.15 = f32[128]{0:T(128)S(1)} all-reduce(f32[128]{0:T(128)S(1)} %psum.14), channel_id=1, replica_groups=mesh['patch'=16,'pix'=2] {'patch'}, use_global_device_ids=true, to_apply=%region_6.7 | all-reduce | flops 128 | bytes 1024 | tf_op jit(solution)/shard_map/psum | solution.py:186
  78.1 0.5 broadcast_multiply_fusion.2
  (50 shorter events, 0.8 us)
Async XLA Ops:
  0.6 14.6 %collective-permute-start.4 = (bf16[48,3,128]{2,0,1:T(8,128)(2,1)}, bf16[48,3,128]{2,0,1:T(8,128)(2,1)S(1)}, u32[]{:S(2)}, u32[]{:S(2)}) collective-permute-start(bf16[48,3,128]{2,0,1:T(8,128)(2,1)} %param.23), channel_id=1, source_target_pairs={{0,2},{2,0},{4,6},{6,4},{8,10},{10,8},{12,14},{14,12},{16,18},{18,... | collective-permute-start | bytes 110600 | tf_op jit(solution)/shard_map/ppermute | solution.py:14
  4.5 0.7 copy-start.3
  4.5 0.7 copy-start.6
  5.2 0.7 copy-start.1
  5.2 0.7 copy-start.2
  5.2 3.7 %collective-permute-start.2 = (f32[7,48]{1,0:T(8,128)S(1)}, f32[7,48]{1,0:T(8,128)S(1)}, u32[]{:S(2)}, u32[]{:S(2)}) collective-permute-start(f32[7,48]{1,0:T(8,128)S(1)} %stack.24), channel_id=1, source_target_pairs={{0,2},{2,0},{4,6},{6,4},{8,10},{10,8},{12,14},{14,12},{16,18},{18,... | collective-permute-start | bytes 4040 | tf_op jit(solution)/shard_map/ppermute | solution.py:14
  5.9 4.6 %collective-permute-start = (f32[5,96]{1,0:T(8,128)S(1)}, f32[5,96]{1,0:T(8,128)S(1)}, u32[]{:S(2)}, u32[]{:S(2)}) collective-permute-start(f32[5,96]{1,0:T(8,128)S(1)} %pad_maximum_fusion.5), channel_id=1, source_target_pairs={{0,8},{2,10},{4,12},{6,14},{8,0},{10,2},{12,4},{14,6},{16,24},{18,... | collective-permute-start | bytes 5768 | tf_op jit(solution)/shard_map/ppermute | solution.py:14
  9.0 4.2 %collective-permute-start.3 = (f32[7,96]{1,0:T(8,128)S(1)}, f32[7,96]{1,0:T(8,128)S(1)}, u32[]{:S(2)}, u32[]{:S(2)}) collective-permute-start(f32[7,96]{1,0:T(8,128)S(1)} %pad_maximum_fusion.6), channel_id=1, source_target_pairs={{0,4},{2,6},{4,0},{6,2},{8,12},{10,14},{12,8},{14,10},{16,20},{18,... | collective-permute-start | bytes 8072 | tf_op jit(solution)/shard_map/ppermute | solution.py:14
  10.6 4.6 %collective-permute-start.1 = (f32[5,192]{1,0:T(8,128)S(1)}, f32[5,192]{1,0:T(8,128)S(1)}, u32[]{:S(2)}, u32[]{:S(2)}) collective-permute-start(f32[5,192]{1,0:T(8,128)S(1)} %pad_maximum_fusion.4), channel_id=1, source_target_pairs={{0,16},{2,18},{4,20},{6,22},{8,24},{10,26},{12,28},{14,30},{16,0},... | collective-permute-start | bytes 11528 | tf_op jit(solution)/shard_map/ppermute | solution.py:14
  13.3 1.9 %copy-start = (bf16[48,3,128]{2,0,1:T(8,128)(2,1)S(1)}, bf16[48,3,128]{2,0,1:T(8,128)(2,1)}, u32[]{:S(2)}) copy-start(bf16[48,3,128]{2,0,1:T(8,128)(2,1)} %param.23) | copy-start | bytes 110596
  15.2 4.4 %collective-permute-start.5 = (bf16[96,3,128]{2,0,1:T(8,128)(2,1)S(1)}, bf16[96,3,128]{2,0,1:T(8,128)(2,1)S(1)}, u32[]{:S(2)}, u32[]{:S(2)}) collective-permute-start(bf16[96,3,128]{2,0,1:T(8,128)(2,1)S(1)} %pad_maximum_fusion.1), channel_id=1, source_target_pairs={{0,4},{2,6},{4,0},{6,2},{8,12},{10,14},{12,8},{14,10},{16,20},{18,... | collective-permute-start | bytes 221192 | tf_op jit(solution)/shard_map/ppermute | solution.py:14
  23.1 5.6 %collective-permute-start.6 = (f32[192,128]{1,0:T(8,128)S(1)}, f32[192,128]{1,0:T(8,128)S(1)}, u32[]{:S(2)}, u32[]{:S(2)}) collective-permute-start(f32[192,128]{1,0:T(8,128)S(1)} %bitcast.102), channel_id=1, source_target_pairs={{0,16},{2,18},{4,20},{6,22},{8,24},{10,26},{12,28},{14,30},{16,0},... | collective-permute-start | bytes 294920 | tf_op jit(solution)/shard_map/ppermute | solution.py:14
  28.7 2.2 %copy-start.7 = (s32[96]{0:T(128)S(1)}, s32[96]{0:T(128)}, u32[]{:S(2)}) copy-start(s32[96]{0:T(128)} %param.17) | copy-start | bytes 1156
  28.8 4.3 %copy-start.4 = (f32[96]{0:T(128)S(1)}, f32[96]{0:T(128)}, u32[]{:S(2)}) copy-start(f32[96]{0:T(128)} %param.16) | copy-start | bytes 1156
  28.8 4.2 %copy-start.5 = (f32[96]{0:T(128)S(1)}, f32[96]{0:T(128)}, u32[]{:S(2)}) copy-start(f32[96]{0:T(128)} %param.15) | copy-start | bytes 1156
  28.8 4.2 %collective-permute-start.7 = (f32[96,128]{1,0:T(8,128)S(1)}, f32[96,128]{1,0:T(8,128)S(1)}, u32[]{:S(2)}, u32[]{:S(2)}) collective-permute-start(f32[96,128]{1,0:T(8,128)S(1)} %slice_select_fusion.2), channel_id=1, source_target_pairs={{0,8},{2,10},{4,12},{6,14},{8,0},{10,2},{12,4},{14,6},{16,24},{18,... | collective-permute-start | bytes 147464 | tf_op jit(solution)/shard_map/ppermute | solution.py:14
